TPU v7x, 32 devices: a whole 2x2x4 slice. The times are simulated.
32 devices in a mesh: row: 4 (over z), col: 4 (over y, x), grid: 2 (over core).
Axes of the slice: x: 2, y: 2, z: 4, core: 2. Of those that a mesh axis runs over, the one named last changes fastest.
Arguments:
- density: bfloat16 [2, 4, 4, 128, 1024], P(None, 'row', None, 'grid', 'col'), may hold values from -0.01171875 to 0.01171875
- basis_values: bfloat16 [16, 256, 512], P(('row', 'col'), 'grid'), may hold values from -6 to 6
- quad_weight: float32 [16, 256], P(('row', 'col'), 'grid'), may hold values from 0.01 to 0.1
- screen: int32 [16, 256], P(('row', 'col'), 'grid'), may hold values 0 or 1
- tile_list: int32 [16, 4], replicated, may hold values from 0 to 7, as said below
Outputs:
- potential_first: bfloat16 [2, 4, 4, 128, 1024], P(None, 'row', None, 'grid', 'col')
- potential_second: bfloat16 [2, 4, 4, 128, 1024], P(None, 'row', None, 'grid', 'col')
Inputs may be any that keep to these rules, and one draw needn't show every extreme that they name: `tile_list`: the 4 tile indices of a batch have distinct remainders modulo 4.
All inputs are finite; a program needn't handle non-finite values. No bound on the sum of `screen` on one device may be relied on, other than what follows from the above.
Results may differ from a plain program's by a relative error of at most 0.014.
Values may be sent and summed in bfloat16 or wider, within the bound.
A program may use at most 64 MiB of HBM per device.

v0:
```python
import jax
import jax.numpy as jnp
from jax import lax
from jax.sharding import PartitionSpec as P

MIXING = 0.001


def local_potential(densities):
    total_density = densities[:, 0:1]
    spin_density = densities[:, 1:4]
    first_part = total_density / jnp.sqrt(1.0 + total_density * total_density)
    spin_norm = jnp.sqrt(1.0 + jnp.sum(spin_density * spin_density, axis=1, keepdims=True))
    return jnp.concatenate([first_part, spin_density / spin_norm], axis=1)


def build(density, basis_values, point_weight, tile_list):
    n_row = lax.axis_size("row")
    n_col = lax.axis_size("col")
    n_grid = lax.axis_size("grid")
    my_row = lax.axis_index("row")
    my_col = lax.axis_index("col")
    per_batch = tile_list.shape[1]
    row_tiles = density.shape[0]
    components = density.shape[2]
    half_tile = density.shape[3]
    tile_width = half_tile * n_grid
    span = per_batch * tile_width
    strip = lax.all_gather(density, "col", axis=4, tiled=True)
    n_tiles = strip.shape[4] // tile_width
    tile_blocks = strip.reshape(row_tiles, components, half_tile, n_tiles, tile_width)
    peer_lists = lax.dynamic_index_in_dim(
        tile_list.reshape(n_row, n_col, per_batch), my_col, axis=1, keepdims=False
    )
    matches = peer_lists % n_row == my_row
    present = jnp.any(matches, axis=1)
    peer_multiple = jnp.sum(jnp.where(matches, peer_lists // n_row, 0), axis=1)

    def pack(multiple, columns):
        row_block = lax.dynamic_index_in_dim(tile_blocks, multiple, 0, keepdims=False)
        return jnp.take(row_block, columns, axis=2)

    payload = jax.vmap(pack)(peer_multiple, peer_lists).reshape(n_row, components, half_tile, span)
    own_list = lax.dynamic_index_in_dim(peer_lists, my_row, 0, keepdims=False)
    residue = own_list % n_row
    arrived = lax.all_to_all(payload, "row", split_axis=0, concat_axis=0, tiled=True)
    own_half = jnp.take(arrived, residue, axis=0)
    gathered_rows = lax.all_gather(own_half, "grid", axis=2, tiled=True)
    blocks = [gathered_rows[:, comp].reshape(span, span) for comp in range(components)]
    samples = basis_values[0]
    samples_wide = samples.astype(jnp.float32)
    densities = jnp.stack(
        [
            jnp.sum(
                jnp.dot(samples, blocks[comp], preferred_element_type=jnp.float32) * samples_wide,
                axis=1,
            )
            for comp in range(components)
        ],
        axis=1,
    )
    potential_scale = point_weight[:, None] * local_potential(densities)
    slabs = []
    for comp in range(components):
        weighted = (samples_wide * potential_scale[:, comp : comp + 1]).astype(jnp.bfloat16)
        partial_value = lax.dot_general(
            samples, weighted, (((0,), (0,)), ((), ())), preferred_element_type=jnp.float32
        )
        slabs.append(partial_value.astype(jnp.bfloat16).reshape(per_batch, n_grid, half_tile, span))
    rounded = jnp.stack(slabs, axis=2)
    pick_multiple = present[:, None] & (peer_multiple[:, None] == jnp.arange(row_tiles)[None, :])
    pick_columns = peer_lists[:, :, None] == jnp.arange(n_tiles)[None, None, :]
    placing = (pick_multiple[:, :, None, None] & pick_columns[:, None, :, :]).astype(jnp.bfloat16)
    outgoing = (
        jnp.zeros((n_row, n_grid, components, half_tile, span), jnp.bfloat16)
        .at[residue]
        .set(rounded)
    )
    outgoing = outgoing.reshape(n_row * n_grid, components, half_tile, span)
    incoming = lax.all_to_all(outgoing, ("row", "grid"), split_axis=0, concat_axis=0, tiled=True)
    incoming = incoming.reshape(n_row * n_grid, components, half_tile, per_batch, tile_width)
    doubled_placing = jnp.broadcast_to(placing[:, None], (n_row, n_grid) + placing.shape[1:])
    doubled_placing = doubled_placing.reshape((n_row * n_grid,) + placing.shape[1:])
    summed = jnp.einsum(
        "qkst,qcasb->kcatb", doubled_placing, incoming, preferred_element_type=jnp.float32
    )
    summed = summed.reshape(row_tiles, components, half_tile, n_tiles * tile_width)
    owned = lax.psum_scatter(summed.astype(jnp.bfloat16), "col", scatter_dimension=3, tiled=True)
    return owned[:, None]


def body(density, basis_values, quad_weight, screen, tile_list):
    point_weight = quad_weight[0] * screen[0].astype(jnp.float32)
    potential_first = build(density, basis_values, point_weight, tile_list)
    updated = (density.astype(jnp.float32) + MIXING * potential_first.astype(jnp.float32)).astype(
        jnp.bfloat16
    )
    potential_second = build(updated, basis_values, point_weight, tile_list)
    return (potential_first, potential_second)


def solution(mesh):
    in_specs = (
        P(None, "row", None, "grid", "col"),
        P(("row", "col"), "grid", None),
        P(("row", "col"), "grid"),
        P(("row", "col"), "grid"),
        P(),
    )
    out_specs = (P(None, "row", None, "grid", "col"), P(None, "row", None, "grid", "col"))
    return jax.shard_map(body, mesh=mesh, in_specs=in_specs, out_specs=out_specs, check_vma=False)
```

profile of v0, /device:TPU:0, one launch (start us, length us, event | category | flops | bytes accessed | tf_op | source)
XLA Modules:
  0.0 361.2 jit_solution(1640813600097828877)
XLA Ops:
  7.2 0.7 all-gather.5.cloned.1.call-update
  7.9 0.8 reshape.300
  9.5 29.5 %all-gather.5.cloned.1.call-done = bf16[2,1,4,64,1024]{4,3,2,1,0:T(8,128)(2,1)} async-done(((bf16[2,1,4,64,256]{4,3,2,1,0:T(8,128)(2,1)}), bf16[2,1,4,64,1024]{4,3,2,1,0:T(8,128)(2,1)}) %all-gather.5.cloned.1.call-update) | async-done | bytes 1048592 | tf_op jit(solution)/shard_map/all_gather | solution.py:29
  38.9 1.5 copy.50
  40.7 1.0 gather_fusion
  41.7 0.8 gather_fusion.2
  42.4 0.9 fusion.31
  43.3 1.2 reshape.302
  44.6 4.6 %all-to-all-start = ((bf16[4,4,64,512]{3,2,1,0:T(8,128)(2,1)}), bf16[4,4,64,512]{3,2,1,0:T(8,128)(2,1)S(1)}, u32[]{:S(2)}, u32[]{:S(2)}) async-start(bf16[4,4,64,512]{3,2,1,0:T(8,128)(2,1)} %reshape.302), calls=%async_computation | async-start | bytes 2097152 | tf_op jit(solution)/shard_map/all_to_all | solution.py:46
  49.2 25.5 %all-to-all-done = bf16[4,4,64,512]{3,2,1,0:T(8,128)(2,1)S(1)} async-done(((bf16[4,4,64,512]{3,2,1,0:T(8,128)(2,1)}), bf16[4,4,64,512]{3,2,1,0:T(8,128)(2,1)S(1)}, u32[]{:S(2)}, u32[]{:S(2)}) %all-to-all-start) | async-done | bytes 1048608 | tf_op jit(solution)/shard_map/all_to_all | solution.py:46
  74.7 0.6 gather_fusion.3
  75.4 1.1 broadcast_select_fusion.1
  76.7 8.7 %all-gather.7.cloned.1.call-done = bf16[4,4,128,512]{3,2,1,0:T(8,128)(2,1)} async-done(((bf16[4,4,64,512]{3,2,1,0:T(8,128)(2,1)}), bf16[4,4,128,512]{3,2,1,0:T(8,128)(2,1)}) %all-gather.7.cloned.1.call-update) | async-done | bytes 2097168 | tf_op jit(solution)/shard_map/all_gather | solution.py:48
  85.4 1.7 fusion.103
  87.1 0.4 fusion.22
  87.5 0.4 fusion.25
  87.9 0.4 fusion.24
  90.4 1.6 broadcast.228.clone
  92.0 5.1 %scatter_fusion = bf16[4,2,4,64,512]{4,3,2,1,0:T(8,128)(2,1)} fusion(bf16[4,2,4,64,512]{4,3,2,1,0:T(8,128)(2,1)} %broadcast.228.clone, s32[4]{0:T(128)S(1)} %get-tuple-element.25, bf16[4,2,4,64,512]{4,3,2,1,0:T(8,128)(2,1)S(1)} %pad_maximum_fusion), kind=kCustom, calls=%fused_computation.6 | custom fusion | bytes 6291472 | tf_op jit(solution)/shard_map/scatter | solution.py:77
  97.1 4.9 %all-to-all-start.1 = ((bf16[8,4,64,512]{3,2,1,0:T(8,128)(2,1)}), bf16[8,4,64,512]{3,2,1,0:T(8,128)(2,1)S(1)}, u32[]{:S(2)}, u32[]{:S(2)}) async-start(bf16[8,4,64,512]{3,2,1,0:T(8,128)(2,1)} %bitcast.41), calls=%async_computation.1 | async-start | bytes 4194304 | tf_op jit(solution)/shard_map/all_to_all | solution.py:80
  102.3 48.7 %all-to-all-done.1 = bf16[8,4,64,512]{3,2,1,0:T(8,128)(2,1)S(1)} async-done(((bf16[8,4,64,512]{3,2,1,0:T(8,128)(2,1)}), bf16[8,4,64,512]{3,2,1,0:T(8,128)(2,1)S(1)}, u32[]{:S(2)}, u32[]{:S(2)}) %all-to-all-start.1) | async-done | bytes 2097184 | tf_op jit(solution)/shard_map/all_to_all | solution.py:80
  151.0 2.1 reshape.304
  153.1 2.7 fusion.8
  156.1 1.3 copy.24
  157.5 26.9 %reduce-scatter.3.cloned.1.call-done = bf16[2,4,64,256]{3,2,1,0:T(8,128)(2,1)} async-done(((bf16[2,4,64,1024]{3,2,1,0:T(8,128)(2,1)}), bf16[2,4,64,256]{3,2,1,0:T(8,128)(2,1)}) %reduce-scatter.3.cloned.1.call-update) | async-done | bytes 262160 | tf_op jit(solution)/shard_map/reduce_scatter | solution.py:88
  184.3 1.7 fusion.32
  186.1 26.8 %all-gather.9.cloned.1.call-done = bf16[2,1,4,64,1024]{4,3,2,0,1:T(8,128)(2,1)} async-done(((bf16[2,1,4,64,256]{4,3,2,0,1:T(8,128)(2,1)}), bf16[2,1,4,64,1024]{4,3,2,0,1:T(8,128)(2,1)}) %all-gather.9.cloned.1.call-update) | async-done | bytes 1048592 | tf_op jit(solution)/shard_map/all_gather | solution.py:29
  213.0 1.5 copy.51
  214.7 1.0 gather_fusion.1
  215.7 0.8 gather_fusion.4
  216.5 0.9 fusion.30
  217.4 0.4 reshape.307
  217.8 30.0 %all_to_all.20 = bf16[4,4,64,512]{3,2,1,0:T(8,128)(2,1)S(1)} all-to-all(bf16[4,4,64,512]{3,2,1,0:T(8,128)(2,1)S(1)} %reshape.307), channel_id=1, replica_groups=mesh['row'=4,'col'=4,'grid'=2] {'row'}, dimensions={0} | all-to-all | bytes 2097152 | tf_op jit(solution)/shard_map/all_to_all | solution.py:46
  247.8 0.6 gather_fusion.5
  248.4 1.1 broadcast_select_fusion
  249.8 8.6 %all-gather.11.cloned.1.call-done = bf16[4,4,128,512]{3,2,1,0:T(8,128)(2,1)} async-done(((bf16[4,4,64,512]{3,2,1,0:T(8,128)(2,1)}), bf16[4,4,128,512]{3,2,1,0:T(8,128)(2,1)}) %all-gather.11.cloned.1.call-update) | async-done | bytes 2097168 | tf_op jit(solution)/shard_map/all_gather | solution.py:48
  258.4 1.7 fusion.102
  260.1 0.4 fusion.26
  260.5 0.4 fusion.29
  260.8 0.4 fusion.28
  261.2 0.4 fusion.27
  263.1 1.6 pad_maximum_fusion.1
  265.0 3.3 scatter_fusion.1
  268.3 53.8 %all_to_all.21 = bf16[8,4,64,512]{3,2,1,0:T(8,128)(2,1)} all-to-all(bf16[8,4,64,512]{3,2,1,0:T(8,128)(2,1)S(1)} %bitcast.340), channel_id=1, replica_groups=mesh['row'=4,'col'=4,'grid'=2] {'row','grid'}, dimensions={0} | all-to-all | bytes 4194304 | tf_op jit(solution)/shard_map/all_to_all | solution.py:80
  322.1 2.5 reshape.309
  324.6 1.1 fusion.11
  326.0 1.3 copy.34
  327.3 27.0 %reduce-scatter.5.cloned.1.call-done = bf16[2,4,64,256]{3,2,1,0:T(8,128)(2,1)} async-done(((bf16[2,4,64,1024]{3,2,1,0:T(8,128)(2,1)}), bf16[2,4,64,256]{3,2,1,0:T(8,128)(2,1)}) %reduce-scatter.5.cloned.1.call-update) | async-done | bytes 262160 | tf_op jit(solution)/shard_map/reduce_scatter | solution.py:88
  (63 shorter events, 6.7 us)
Async XLA Ops:
  7.2 31.8 %all-gather.5.cloned.1.call-start = ((), (), s32[]{:S(2)}) async-start(), calls=%async_computation.6 | async-start | bytes 1310720 | tf_op jit(solution)/shard_map/all_gather | solution.py:29
  44.6 30.2 %all-to-all-start = ((bf16[4,4,64,512]{3,2,1,0:T(8,128)(2,1)}), bf16[4,4,64,512]{3,2,1,0:T(8,128)(2,1)S(1)}, u32[]{:S(2)}, u32[]{:S(2)}) async-start(bf16[4,4,64,512]{3,2,1,0:T(8,128)(2,1)} %reshape.302), calls=%async_computation | async-start | bytes 2097152 | tf_op jit(solution)/shard_map/all_to_all | solution.py:46
  49.2 36.2 %all-gather.7.cloned.1.call-start = ((), (), s32[]{:S(2)}) async-start(), calls=%async_computation.7 | async-start | bytes 3145728 | tf_op jit(solution)/shard_map/all_gather | solution.py:48
  75.3 1.2 copy-start
  75.4 1.3 copy-start.2
  75.4 1.3 copy-start.3
  97.1 53.9 %all-to-all-start.1 = ((bf16[8,4,64,512]{3,2,1,0:T(8,128)(2,1)}), bf16[8,4,64,512]{3,2,1,0:T(8,128)(2,1)S(1)}, u32[]{:S(2)}, u32[]{:S(2)}) async-start(bf16[8,4,64,512]{3,2,1,0:T(8,128)(2,1)} %bitcast.41), calls=%async_computation.1 | async-start | bytes 4194304 | tf_op jit(solution)/shard_map/all_to_all | solution.py:80
  102.0 82.4 %reduce-scatter.3.cloned.1.call-start = ((), (), s32[]{:S(2)}) async-start(), calls=%async_computation.8 | async-start | bytes 1310720 | tf_op jit(solution)/shard_map/reduce_scatter | solution.py:88
  156.1 28.2 %copy-start.1 = (bf16[2,1,4,64,256]{4,3,2,1,0:T(8,128)(2,1)S(1)}, bf16[2,1,4,64,256]{4,3,2,1,0:T(8,128)(2,1)}, u32[]{:S(2)}) copy-start(bf16[2,1,4,64,256]{4,3,2,1,0:T(8,128)(2,1)} %param.9) | copy-start | bytes 786436
  157.4 55.5 %all-gather.9.cloned.1.call-start = ((), (), s32[]{:S(2)}) async-start(), calls=%async_computation.9 | async-start | bytes 1310720 | tf_op jit(solution)/shard_map/all_gather | solution.py:29
  186.1 72.3 %all-gather.11.cloned.1.call-start = ((), (), s32[]{:S(2)}) async-start(), calls=%async_computation.10 | async-start | bytes 3145728 | tf_op jit(solution)/shard_map/all_gather | solution.py:48
  249.6 104.7 %reduce-scatter.5.cloned.1.call-start = ((), (), s32[]{:S(2)}) async-start(), calls=%async_computation.11 | async-start | bytes 1310720 | tf_op jit(solution)/shard_map/reduce_scatter | solution.py:88
Sparse Core Ops, SparseCore 0:
  9.8 29.0 all-gather.4
  76.7 8.6 all-gather.6
  157.5 26.7 reduce-scatter.2
  186.6 26.3 all-gather.8
  249.7 8.6 all-gather.10
  327.5 26.7 reduce-scatter.4
where the time goes:
time: 362 us; the launch traced here: 361 us
  waiting for transfers between devices  202 us (56%)
  blocking collectives  83.8 us (23%)
  local copies, waits for them, and re-layouts  32.7 us (9%)
  between operations  14.5 us (4%)
  starting transfers between devices  9.86 us (3%)
  matrix products  9.63 us (3%)
  other arithmetic  8.28 us (2%)
    all_gather x2, waiting for transfers between devices, build(): strip = lax.all_gather(density, 'col', axis=4, tiled=True)  56.3 us
    reduce_scatter x2, waiting for transfers between devices, build(): lax.psum_scatter(summed.astype(jnp.bfloat16), 'col', scatter_dimension=3,...  53.8 us
    all_to_all x1, blocking collectives, build(): lax.all_to_all(outgoing, ('row', 'grid'), split_axis=0, concat_axis=0, ti...  53.8 us
    all_to_all x1, waiting for transfers between devices, build(): lax.all_to_all(outgoing, ('row', 'grid'), split_axis=0, concat_axis=0, ti...  48.7 us
    all_to_all x1, blocking collectives, build(): lax.all_to_all(payload, 'row', split_axis=0, concat_axis=0, tiled=True)  30 us
    all_to_all x1, waiting for transfers between devices, build(): lax.all_to_all(payload, 'row', split_axis=0, concat_axis=0, tiled=True)  25.5 us
    all_gather x2, waiting for transfers between devices, build(): gathered_rows = lax.all_gather(own_half, 'grid', axis=2, tiled=True)  17.3 us
    scatter x2, local copies, waits for them, and re-layouts, build(): outgoing = jnp.zeros((n_row, n_grid, components, half_tile, span), jnp.bf...  8.39 us
  transfers between devices with their start and end apart: 8, of which 8 were waited for; matrix products, arithmetic and copies ran while one was open for 1% of the time, Pallas kernels for 0%

commit v1 on v0

v1 whole, which is shorter than its diff:
```python
import functools

import jax
import jax.numpy as jnp
from jax import lax
from jax.experimental import pallas as pl
from jax.experimental.pallas import tpu as pltpu
from jax.sharding import PartitionSpec as P

MIXING = 0.001
AXES = ("row", "col", "grid")


def tile_rows(density_ref, comp):
    return jnp.concatenate([density_ref[k, comp] for k in range(density_ref.shape[0])], axis=0)


def density_kernel(rows_ref, cols_ref, density_ref, out_ref, flipped):
    components = density_ref.shape[1]
    slabs, _, points = rows_ref.shape

    @pl.when(pl.program_id(0) == 0)
    def _():
        for comp in range(components):
            block = tile_rows(density_ref, comp).astype(jnp.float32)
            flipped[comp] = block.T.astype(jnp.bfloat16)

    for slab in range(0, slabs, 2):
        rows = jnp.concatenate([rows_ref[slab], rows_ref[slab + 1]], axis=1)
        cols = jnp.concatenate([cols_ref[slab], cols_ref[slab + 1]], axis=1).astype(jnp.float32)
        for comp in range(components):
            contracted = jnp.dot(flipped[comp], rows, preferred_element_type=jnp.float32)
            total = jnp.sum(contracted * cols, axis=0, keepdims=True)
            out_ref[slab, comp : comp + 1, :] = total[:, :points]
            out_ref[slab + 1, comp : comp + 1, :] = total[:, points:]


def potential_kernel(rows_ref, cols_ref, dens_ref, weight_ref, density_ref, out_ref, updated_ref, total):
    row_tiles, components, half_tile, _ = density_ref.shape
    slabs = rows_ref.shape[0]

    @pl.when(pl.program_id(0) == 0)
    def _():
        total[...] = jnp.zeros_like(total)

    rows_wide = [rows_ref[slab].astype(jnp.float32) for slab in range(slabs)]
    cols = jnp.concatenate([cols_ref[slab] for slab in range(slabs)], axis=1)
    dens = dens_ref[...]
    first = dens[:, 0:1, :]
    spin = dens[:, 1:, :]
    spin_norm = jnp.sqrt(1.0 + jnp.sum(spin * spin, axis=1, keepdims=True))
    weight = weight_ref[...]
    scales = [weight * (first / jnp.sqrt(1.0 + first * first))]
    scales += [weight * (dens[:, comp : comp + 1, :] / spin_norm) for comp in range(1, components)]
    for comp in range(components):
        weighted = jnp.concatenate(
            [(rows_wide[slab] * scales[comp][slab]).astype(jnp.bfloat16) for slab in range(slabs)], axis=1
        )
        total[comp] += lax.dot_general(
            weighted, cols, (((1,), (1,)), ((), ())), preferred_element_type=jnp.float32
        )

    @pl.when(pl.program_id(0) == pl.num_programs(0) - 1)
    def _():
        for comp in range(components):
            rounded = total[comp].astype(jnp.bfloat16)
            for k in range(row_tiles):
                piece = rounded[k * half_tile : (k + 1) * half_tile]
                out_ref[k, comp] = piece
                updated_ref[k, comp] = (
                    density_ref[k, comp].astype(jnp.float32) + MIXING * piece.astype(jnp.float32)
                ).astype(jnp.bfloat16)


def chunk_of(slabs):
    return 8 if slabs % 8 == 0 else 2


def local_densities(rows, cols, density):
    slabs, height, points = rows.shape
    width = cols.shape[1]
    components = density.shape[1]
    chunk = chunk_of(slabs)
    return pl.pallas_call(
        density_kernel,
        grid=(slabs // chunk,),
        out_shape=jax.ShapeDtypeStruct((slabs, components, points), jnp.float32),
        in_specs=[
            pl.BlockSpec((chunk, height, points), lambda i: (i, 0, 0)),
            pl.BlockSpec((chunk, width, points), lambda i: (i, 0, 0)),
            pl.BlockSpec(density.shape, lambda i: (0, 0, 0, 0)),
        ],
        out_specs=pl.BlockSpec((chunk, components, points), lambda i: (i, 0, 0)),
        scratch_shapes=[pltpu.VMEM((components, width, height), jnp.bfloat16)],
    )(rows, cols, density)


def local_potential(rows, cols, dens, weight, density):
    slabs, height, points = rows.shape
    width = cols.shape[1]
    components = density.shape[1]
    chunk = chunk_of(slabs)
    whole = pl.BlockSpec(density.shape, lambda i: (0, 0, 0, 0))
    shape = jax.ShapeDtypeStruct(density.shape, density.dtype)
    return pl.pallas_call(
        potential_kernel,
        grid=(slabs // chunk,),
        out_shape=(shape, shape),
        in_specs=[
            pl.BlockSpec((chunk, height, points), lambda i: (i, 0, 0)),
            pl.BlockSpec((chunk, width, points), lambda i: (i, 0, 0)),
            pl.BlockSpec((chunk, components, points), lambda i: (i, 0, 0)),
            pl.BlockSpec((chunk, 1, points), lambda i: (i, 0, 0)),
            whole,
        ],
        out_specs=(whole, whole),
        scratch_shapes=[pltpu.VMEM((components, height, width), jnp.float32)],
    )(rows, cols, dens, weight, density)


def body(density, basis_values, quad_weight, screen, tile_list):
    n_row = lax.axis_size("row")
    n_grid = lax.axis_size("grid")
    my_row = lax.axis_index("row")
    my_col = lax.axis_index("col")
    my_grid = lax.axis_index("grid")
    density = density[:, 0]
    row_tiles, components, half_tile, width = density.shape
    tile_width = half_tile * n_grid
    own_tiles = width // tile_width
    batches, per_batch = tile_list.shape
    points = basis_values.shape[1]
    slabs = batches * n_grid

    turned = basis_values[0].T
    gathered = lax.all_gather(turned, AXES, axis=0, tiled=False)
    weight = quad_weight[0] * screen[0].astype(jnp.float32)
    weight = lax.all_gather(weight, AXES, axis=0, tiled=False)[:, None, :]

    lists = jnp.repeat(tile_list, n_grid, axis=0)
    split = gathered.reshape(slabs, per_batch, tile_width, points)
    half = lax.dynamic_slice_in_dim(split, my_grid * half_tile, half_tile, axis=2)

    def pick(source, wanted):
        result = jnp.zeros((slabs,) + source.shape[2:], source.dtype)
        for place in range(per_batch):
            match = (lists[:, place] == wanted)[:, None, None]
            result = jnp.where(match, source[:, place], result)
        return result

    rows = jnp.concatenate([pick(half, k * n_row + my_row) for k in range(row_tiles)], axis=1)
    cols = jnp.concatenate([pick(split, my_col * own_tiles + j) for j in range(own_tiles)], axis=1)

    dens = lax.psum(local_densities(rows, cols, density), AXES)
    potential_first, updated = local_potential(rows, cols, dens, weight, density)
    dens = lax.psum(local_densities(rows, cols, updated), AXES)
    potential_second, _ = local_potential(rows, cols, dens, weight, updated)
    return (potential_first[:, None], potential_second[:, None])


def solution(mesh):
    in_specs = (
        P(None, "row", None, "grid", "col"),
        P(("row", "col"), "grid", None),
        P(("row", "col"), "grid"),
        P(("row", "col"), "grid"),
        P(),
    )
    out_specs = (P(None, "row", None, "grid", "col"), P(None, "row", None, "grid", "col"))
    return jax.shard_map(body, mesh=mesh, in_specs=in_specs, out_specs=out_specs, check_vma=False)
```

time: 362 us -> 352 us (0.972)
  waiting for transfers between devices: 202 us -> 263 us
  blocking collectives: 83.8 us -> 41.5 us
  local copies, waits for them, and re-layouts: 32.7 us -> 2.44 us
  Pallas kernels: 0 us -> 22.5 us
  starting transfers between devices: 9.86 us -> 0.12 us
  matrix products: 9.63 us -> 0 us
    psum x0 -> x2, waiting for transfers between devices: none -> 197 us  [the longest x1 121 us: body(): dens = lax.psum(local_densities(rows, cols, updated), AXES)]
    all_to_all x2 -> x0, blocking collectives: 83.8 us -> none  [the longest x1 53.8 us: build(): lax.all_to_all(outgoing, ('row', 'grid'), split_axis=0, concat_axis=0, ti...]
    all_to_all x2 -> x0, waiting for transfers between devices: 74.2 us -> none  [the longest x1 48.7 us: build(): lax.all_to_all(outgoing, ('row', 'grid'), split_axis=0, concat_axis=0, ti...]
    reduce_scatter x2 -> x0, waiting for transfers between devices: 53.8 us -> none  [build(): lax.psum_scatter(summed.astype(jnp.bfloat16), 'col', scatter_dimension=3,...]
    all_gather x0 -> x1, blocking collectives: none -> 41.5 us  [body(): weight = lax.all_gather(weight, AXES, axis=0, tiled=False)[:, None, :]]
    pallas_call x0 -> x4, Pallas kernels: none -> 22.5 us  [the longest x2 12 us: local_potential(): pl.pallas_call(potential_kernel, grid=(slabs // chunk,), out_shape=(shape...]
    dot_general x18 -> x0, matrix products: 9.63 us -> none  [the longest x2 3.85 us: build(): jnp.einsum('qkst,qcasb->kcatb', doubled_placing, incoming, preferred_elem...]
    all_to_all x2 -> x0, starting transfers between devices: 9.47 us -> none  [the longest x1 4.88 us: build(): lax.all_to_all(outgoing, ('row', 'grid'), split_axis=0, concat_axis=0, ti...]
  transfers between devices with their start and end apart: 8 -> 3, of which waited for: 8 -> 3; matrix products, arithmetic and copies ran while one was open for 1% -> 0% of each run, Pallas kernels for 0% -> 0%
where the time goes in v1:
time: 352 us; the launch traced here: 350 us
  waiting for transfers between devices  263 us (75%)
  blocking collectives  41.5 us (12%)
  Pallas kernels  22.5 us (6%)
  between operations  13.8 us (4%)
  other arithmetic  6.3 us (2%)
    psum x1, waiting for transfers between devices, body(): dens = lax.psum(local_densities(rows, cols, updated), AXES)  121 us
    psum x1, waiting for transfers between devices, body(): dens = lax.psum(local_densities(rows, cols, density), AXES)  76.7 us
    all_gather x1, waiting for transfers between devices, body(): gathered = lax.all_gather(turned, AXES, axis=0, tiled=False)  65.6 us
    all_gather x1, blocking collectives, body(): weight = lax.all_gather(weight, AXES, axis=0, tiled=False)[:, None, :]  41.5 us
    pallas_call x2, Pallas kernels, local_potential(): pl.pallas_call(potential_kernel, grid=(slabs // chunk,), out_shape=(shape...  12 us
    pallas_call x2, Pallas kernels, local_densities(): pl.pallas_call(density_kernel, grid=(slabs // chunk,), out_shape=jax.Shap...  10.6 us
  transfers between devices with their start and end apart: 3, of which 3 were waited for; matrix products, arithmetic and copies ran while one was open for 0% of the time, Pallas kernels for 0%

profile of v1, /device:TPU:0, one launch (start us, length us, event | category | flops | bytes accessed | tf_op | source)
XLA Modules:
  0.0 349.8 jit_solution(2659258334879077503)
XLA Ops:
  7.2 0.0 all-gather.4.cloned.1.call-start
  7.2 1.7 copy.20
  8.9 0.0 all-gather.4.cloned.1.call-update
  8.9 0.0 all-reduce.3.cloned.1.call-start
  9.0 0.8 copy.19
  9.7 0.4 compare_reduce_fusion.7
  10.2 65.6 %all-gather.4.cloned.1.call-done = bf16[16384,128]{1,0:T(8,128)(2,1)} async-done(((bf16[512,128]{1,0:T(8,128)(2,1)}), bf16[16384,128]{1,0:T(8,128)(2,1)}) %all-gather.4.cloned.1.call-update) | async-done | bytes 4194320 | tf_op jit(solution)/shard_map/all_gather | solution.py:136
  75.8 0.0 copy-start
  75.8 2.5 select_select_fusion.3
  78.3 1.1 pad_maximum_fusion.1.rows_ref
  79.3 0.0 copy-done
  79.3 0.7 select_select_fusion.1
  80.1 1.6 pad_maximum_fusion.cols_ref
  81.6 0.0 copy-start.1
  81.6 0.0 copy-start.2
  81.6 5.3 %shard_map.68 = f32[32,4,128]{2,1,0:T(4,128)} custom-call(bf16[32,128,128]{2,1,0:T(8,128)(2,1)} %pad_maximum_fusion.1.rows_ref, bf16[32,256,128]{2,1,0:T(8,128)(2,1)} %pad_maximum_fusion.cols_ref, bf16[2,4,64,256]{3,2,1,0:T(8,128)(2,1)} %bitcast.80), custom_call_target="tpu_custom_call" | custom-call | tf_op jit(solution)/shard_map/pallas_call | solution.py:84
  86.9 0.0 all-reduce.3.cloned.1.call-update
  87.0 0.0 all-reduce.5.cloned.1.call-start
  87.0 0.0 copy-done.1
  87.0 0.0 copy-done.2
  87.0 41.5 %all-gather.1.weight_ref = f32[32,1,128]{2,1,0:T(1,128)} all-gather(f32[1,1,128]{2,1,0:T(1,128)S(1)} %multiply_bitcast_fusion), channel_id=1, replica_groups=mesh['row'=4,'col'=4,'grid'=2] {'row','col','grid'}, dimensions={0}, use_global_device_ids=true | all-gather | bytes 16896 | tf_op jit(solution)/shard_map/all_gather | solution.py:138
  128.6 76.7 %all-reduce.3.cloned.1.call-done.dens_ref = f32[32,4,128]{2,1,0:T(4,128)} async-done(((f32[32,4,128]{2,1,0:T(4,128)}), f32[32,4,128]{2,1,0:T(4,128)}) %all-reduce.3.cloned.1.call-update) | async-done | bytes 65552 | tf_op jit(solution)/shard_map/psum | solution.py:154
  205.3 6.0 %shard_map.69 = (bf16[2,4,64,256]{3,2,1,0:T(8,128)(2,1)}, bf16[2,4,64,256]{3,2,1,0:T(8,128)(2,1)}) custom-call(bf16[32,128,128]{2,1,0:T(8,128)(2,1)} %pad_maximum_fusion.1.rows_ref, bf16[32,256,128]{2,1,0:T(8,128)(2,1)} %pad_maximum_fusion.cols_ref, f32[32,4,128]{2,1,0:T(4,128)} %all-reduce.3.cloned.1.call-done.dens_ref, ...), custom_call_target="tpu_custom_call" | custom-call | tf_op jit(solution)/shard_map/pallas_call | solution.py:105
  211.3 5.3 %shard_map.70 = f32[32,4,128]{2,1,0:T(4,128)} custom-call(bf16[32,128,128]{2,1,0:T(8,128)(2,1)} %pad_maximum_fusion.1.rows_ref, bf16[32,256,128]{2,1,0:T(8,128)(2,1)} %pad_maximum_fusion.cols_ref, bf16[2,4,64,256]{3,2,1,0:T(8,128)(2,1)} %get-tuple-element.6.density_ref), custom_call_target="tpu_custom_call" | custom-call | tf_op jit(solution)/shard_map/pallas_call | solution.py:84
  216.6 0.0 all-reduce.5.cloned.1.call-update
  216.6 120.7 %all-reduce.5.cloned.1.call-done.dens_ref = f32[32,4,128]{2,1,0:T(4,128)} async-done(((f32[32,4,128]{2,1,0:T(4,128)}), f32[32,4,128]{2,1,0:T(4,128)}) %all-reduce.5.cloned.1.call-update) | async-done | bytes 65552 | tf_op jit(solution)/shard_map/psum | solution.py:156
  337.4 6.0 %shard_map.71 = (bf16[2,4,64,256]{3,2,1,0:T(8,128)(2,1)}, bf16[2,4,64,256]{3,2,1,0:T(8,128)(2,1)}) custom-call(bf16[32,128,128]{2,1,0:T(8,128)(2,1)} %pad_maximum_fusion.1.rows_ref, bf16[32,256,128]{2,1,0:T(8,128)(2,1)} %pad_maximum_fusion.cols_ref, f32[32,4,128]{2,1,0:T(4,128)} %all-reduce.5.cloned.1.call-done.dens_ref, ...), custom_call_target="tpu_custom_call" | custom-call | tf_op jit(solution)/shard_map/pallas_call | solution.py:105
  (2 shorter events, 0.0 us)
Async XLA Ops:
  7.2 68.6 %all-gather.4.cloned.1.call-start = ((), (), s32[]{:S(2)}) async-start(), calls=%async_computation.2 | async-start | bytes 4325376 | tf_op jit(solution)/shard_map/all_gather | solution.py:136
  8.9 196.4 %all-reduce.3.cloned.1.call-start = ((), (), s32[]{:S(2)}) async-start(), calls=%async_computation | async-start | bytes 131072 | tf_op jit(solution)/shard_map/psum | solution.py:154
  75.8 3.6 %copy-start = (bf16[16384,128]{1,0:T(8,128)(2,1)S(1)}, bf16[16384,128]{1,0:T(8,128)(2,1)}, u32[]{:S(2)}) copy-start(bf16[16384,128]{1,0:T(8,128)(2,1)} %all-gather.4.cloned.1.call-done) | copy-start | bytes 12582916
  81.6 5.4 %copy-start.1 = (f32[1,128]{1,0:T(1,128)S(1)}, f32[1,128]{1,0:T(1,128)}, u32[]{:S(2)}) copy-start(f32[1,128]{1,0:T(1,128)} %param.7) | copy-start | bytes 1540
  81.6 5.4 %copy-start.2 = (s32[1,128]{1,0:T(1,128)S(1)}, s32[1,128]{1,0:T(1,128)}, u32[]{:S(2)}) copy-start(s32[1,128]{1,0:T(1,128)} %param.8) | copy-start | bytes 1540
  87.0 250.4 %all-reduce.5.cloned.1.call-start = ((), (), s32[]{:S(2)}) async-start(), calls=%async_computation.1 | async-start | bytes 131072 | tf_op jit(solution)/shard_map/psum | solution.py:156
Sparse Core Ops, SparseCore 0:
  11.4 64.3 all-gather.3
  87.1 118.1 all-reduce.2
  216.7 120.5 all-reduce.4
